TPU v7x, 8 devices: a whole 2x2x1 slice. The times are simulated.
8 devices in a mesh: dp: 1 (over z), tp: 2 (over y), cp: 4 (over x, core).
Axes of the slice: x: 2, y: 2, z: 1, core: 2. Of those that a mesh axis runs over, the one named last changes fastest.
Arguments:
- tokens: bfloat16 [2048, 5120], P(('dp', 'tp', 'cp'))
- norm_attn: bfloat16 [2, 5120], replicated
- norm_mlp: bfloat16 [2, 5120], replicated
- w_q: bfloat16 [2, 5120, 32, 128], P(None, None, 'tp')
- w_k: bfloat16 [2, 5120, 1024], P(None, None, 'tp')
- w_v: bfloat16 [2, 5120, 1024], P(None, None, 'tp')
- w_o: bfloat16 [2, 32, 128, 5120], P(None, 'tp')
- w_gate: bfloat16 [2, 5120, 14336], P(None, None, 'tp')
- w_up: bfloat16 [2, 5120, 14336], P(None, None, 'tp')
- w_down: bfloat16 [2, 14336, 5120], P(None, 'tp')
Outputs:
- output: bfloat16 [2048, 5120], P(('dp', 'tp', 'cp'))
All inputs are finite; a program needn't handle non-finite values.
Results may differ from a plain program's by a relative error of at most 0.0167808.
Values are sent between devices in bfloat16 or wider.
A program may use at most 2.25 GiB of HBM per device.

v0:
```python
import math
import jax
import jax.numpy as jnp
from jax import lax
from jax.sharding import PartitionSpec as P, NamedSharding


def rms_norm(hidden, gain):
    hidden_f = hidden.astype(jnp.float32)
    inv_rms = lax.rsqrt(jnp.mean(hidden_f * hidden_f, axis=-1, keepdims=True) + 1e-5)
    return (hidden_f * inv_rms * gain.astype(jnp.float32)).astype(jnp.bfloat16)


def rotary(values, positions):
    half_dim = values.shape[-1] // 2
    inv_freq = 500000.0 ** (-(jnp.arange(half_dim, dtype=jnp.float32) * 2.0 / values.shape[-1]))
    angles = positions.astype(jnp.float32)[:, None] * inv_freq[None, :]
    cos_ang = jnp.cos(angles)[:, None, :]
    sin_ang = jnp.sin(angles)[:, None, :]
    first = values[..., :half_dim]
    second = values[..., half_dim:]
    return jnp.concatenate([first * cos_ang - second * sin_ang, second * cos_ang + first * sin_ang], axis=-1)


def seg_positions(dev_ids, rows, dev_total):
    offset = jnp.arange(rows)
    half_len = rows // 2
    seg_idx = jnp.where(offset < half_len, dev_ids[..., None], 2 * dev_total - 1 - dev_ids[..., None])
    return seg_idx * half_len + offset % half_len


def attend(queries, keys_all, values_all, q_pos, k_pos, block_rows):
    rows, kv_loc, group, head_dim = queries.shape
    scale = 1.0 / math.sqrt(head_dim)
    q_blocks = queries.reshape(rows // block_rows, block_rows, kv_loc, group, head_dim)
    pos_blocks = q_pos.reshape(rows // block_rows, block_rows)

    def one_block(block):
        q_blk, pos_blk = block
        scores = jnp.einsum('bkgd,tkd->bkgt', q_blk, keys_all, preferred_element_type=jnp.float32) * scale
        visible = k_pos[None, None, None, :] <= pos_blk[:, None, None, None]
        scores = jnp.where(visible, scores, -jnp.inf)
        weights = jnp.exp(scores - jnp.max(scores, axis=-1, keepdims=True))
        row_sum = jnp.sum(weights, axis=-1, keepdims=True)
        mixed = jnp.einsum('bkgt,tkd->bkgd', weights.astype(jnp.bfloat16), values_all, preferred_element_type=jnp.float32)
        return (mixed / row_sum).astype(jnp.bfloat16)

    return lax.map(one_block, (q_blocks, pos_blocks)).reshape(rows, kv_loc * group, head_dim)


def solution(mesh):
    tp_size = mesh.shape['tp']
    cp_size = mesh.shape['cp']
    dev_total = tp_size * cp_size
    row_spec = P(('dp', 'tp', 'cp'), None)
    gain_spec = P(None, None)
    q_spec = P(None, None, 'tp', None)
    col_spec = P(None, None, 'tp')
    o_spec = P(None, 'tp', None, None)
    down_spec = P(None, 'tp', None)

    def body(tokens, norm_attn, norm_mlp, w_q, w_k, w_v, w_o, w_gate, w_up, w_down):
        rows = tokens.shape[0]
        heads_loc = w_q.shape[2]
        head_dim = w_q.shape[3]
        kv_cols = w_k.shape[2]
        tp_idx = lax.axis_index('tp')
        cp_idx = lax.axis_index('cp')
        tp_devs = jnp.arange(tp_size) * cp_size + cp_idx
        pos_rows = seg_positions(tp_devs, rows, dev_total).reshape(tp_size * rows)
        key_devs = jnp.arange(cp_size)[:, None] + jnp.arange(tp_size)[None, :] * cp_size
        pos_keys = seg_positions(key_devs, rows, dev_total).reshape(dev_total * rows)
        hidden = tokens
        for layer_idx in range(w_q.shape[0]):
            normed = lax.all_gather(rms_norm(hidden, norm_attn[layer_idx]), 'tp', axis=0, tiled=True)
            q_proj = jnp.einsum('rd,dhe->rhe', normed, w_q[layer_idx], preferred_element_type=jnp.float32)
            queries = rotary(q_proj, pos_rows).astype(jnp.bfloat16)
            wk_loc = w_k[layer_idx]
            wv_loc = w_v[layer_idx]
            if kv_cols >= head_dim:
                kv_loc = kv_cols // head_dim
            else:
                kv_total = kv_cols * tp_size // head_dim
                start = (tp_idx * kv_total // tp_size) * head_dim
                wk_loc = lax.dynamic_slice_in_dim(lax.all_gather(wk_loc, 'tp', axis=1, tiled=True), start, head_dim, axis=1)
                wv_loc = lax.dynamic_slice_in_dim(lax.all_gather(wv_loc, 'tp', axis=1, tiled=True), start, head_dim, axis=1)
                kv_loc = 1
            k_proj = jnp.dot(normed, wk_loc, preferred_element_type=jnp.float32)
            keys_loc = rotary(k_proj.reshape(tp_size * rows, kv_loc, head_dim), pos_rows).astype(jnp.bfloat16)
            values_loc = jnp.dot(normed, wv_loc, preferred_element_type=jnp.float32).astype(jnp.bfloat16).reshape(tp_size * rows, kv_loc, head_dim)
            keys_all = lax.all_gather(keys_loc, 'cp', axis=0, tiled=True)
            values_all = lax.all_gather(values_loc, 'cp', axis=0, tiled=True)
            grouped = queries.reshape(tp_size * rows, kv_loc, heads_loc // kv_loc, head_dim)
            mixed = attend(grouped, keys_all, values_all, pos_rows, pos_keys, rows // 2)
            attn_part = jnp.einsum('rhe,hed->rd', mixed, w_o[layer_idx], preferred_element_type=jnp.float32)
            attn_out = lax.psum_scatter(attn_part, 'tp', scatter_dimension=0, tiled=True)
            hidden_mid = (hidden.astype(jnp.float32) + attn_out).astype(jnp.bfloat16)
            normed_mlp = lax.all_gather(rms_norm(hidden_mid, norm_mlp[layer_idx]), 'tp', axis=0, tiled=True)
            gate_pre = jnp.dot(normed_mlp, w_gate[layer_idx], preferred_element_type=jnp.float32)
            up_proj = jnp.dot(normed_mlp, w_up[layer_idx], preferred_element_type=jnp.float32)
            hidden_act = (jax.nn.silu(gate_pre) * up_proj).astype(jnp.bfloat16)
            mlp_part = jnp.dot(hidden_act, w_down[layer_idx], preferred_element_type=jnp.float32)
            mlp_out = lax.psum_scatter(mlp_part, 'tp', scatter_dimension=0, tiled=True)
            hidden = (hidden_mid.astype(jnp.float32) + mlp_out).astype(jnp.bfloat16)
        return hidden

    return jax.shard_map(
        body,
        mesh=mesh,
        in_specs=(row_spec, gain_spec, gain_spec, q_spec, col_spec, col_spec, o_spec, col_spec, col_spec, down_spec),
        out_specs=row_spec,
        check_vma=False,
    )
```

profile of v0, /device:TPU:0, one launch (start us, length us, event | category | flops | bytes accessed | tf_op | source)
XLA Modules:
  0.0 1417.8 jit_solution(7782466205076287877)
XLA Ops:
  14.5 8.7 slice_bitcast_fusion
  31.8 51.7 %all-gather.9.cloned.1.call-done = bf16[512,5120]{1,0:T(8,128)(2,1)} async-done(((bf16[256,5120]{1,0:T(8,128)(2,1)}), bf16[512,5120]{1,0:T(8,128)(2,1)}) %all-gather.9.cloned.1.call-update) | async-done | bytes 5242896 | tf_op jit(solution)/shard_map/all_gather | solution.py:75
  91.1 28.9 %fusion.150 = (bf16[1,5120,16,128]{3,2,1,0:T(8,128)(2,1)}, bf16[1,5120,16,128]{3,2,1,0:T(8,128)(2,1)}) fusion(bf16[2,5120,16,128]{3,2,1,0:T(8,128)(2,1)} %param.17), kind=kLoop, calls=%fused_computation.159 | loop fusion | bytes 83886080 | tf_op jit(solution)/shard_map/slice | solution.py:76
  120.0 27.6 %copy.67 = bf16[1,5120,16,128]{1,3,2,0:T(8,128)(2,1)} copy(bf16[1,5120,16,128]{3,2,1,0:T(8,128)(2,1)} %get-tuple-element.244) | data formatting | bytes 41943040
  156.3 15.7 %fusion.151 = f32[512,2048]{0,1:S(1)} fusion(bf16[512,5120]{1,0:T(8,128)(2,1)} %all-gather.9.cloned.1.call-done, bf16[5120,2048]{0,1:T(8,128)(2,1)} %bitcast.300), kind=kOutput, calls=%fused_computation.160 | convolution fusion | flops 10737418240 | bytes 30408704
  190.8 58.0 %while.22 = (s32[]{:T(128)}, bf16[4,128,4,4,128]{4,1,0,3,2:T(8,128)(2,1)}, s32[4,128]{1,0:T(4,128)S(1)}, bf16[4,128,4,4,128]{4,1,3,2,0:T(8,128)(2,1)}, bf16[2048...) while((s32[]{:T(128)}, ...), condition=%wide.region_4.5_spmd.clone, body=%wide.region_1.4_spmd.clone.sunk | while | flops 2194409472 | bytes 65089484 | solution.py:48
  248.8 17.3 %fusion.104 = f32[512,5120]{1,0:T(8,128)} fusion(bf16[512,16,128]{2,0,1:T(8,128)(2,1)} %bitcast.11, bf16[2,16,128,5120]{3,2,1,0:T(8,128)(2,1)} %param.20), kind=kOutput, calls=%fused_computation.76 | convolution fusion | flops 10737418240 | bytes 33554432 | tf_op jit(solution)/shard_map/rhe,hed->rd/dot_general | solution.py:95
  267.6 117.9 %reduce-scatter.5.cloned.1.call-done = f32[256,5120]{1,0:T(8,128)} async-done(((f32[512,5120]{1,0:T(8,128)}), f32[256,5120]{1,0:T(8,128)}) %reduce-scatter.5.cloned.1.call-update) | async-done | bytes 5242896 | tf_op jit(solution)/shard_map/reduce_scatter | solution.py:96
  392.8 66.3 %all-gather.15.cloned.1.call-done = bf16[512,5120]{1,0:T(8,128)(2,1)} async-done(((bf16[256,5120]{1,0:T(8,128)(2,1)}), bf16[512,5120]{1,0:T(8,128)(2,1)}) %all-gather.15.cloned.1.call-update) | async-done | bytes 5242896 | tf_op jit(solution)/shard_map/all_gather | solution.py:98
  459.1 49.0 %fusion.82 = f32[512,7168]{1,0:T(8,128)} fusion(bf16[512,5120]{1,0:T(8,128)(2,1)} %all-gather.15.cloned.1.call-done, bf16[2,5120,7168]{2,1,0:T(8,128)(2,1)} %param.21), kind=kOutput, calls=%fused_computation.60 | convolution fusion | flops 37580963840 | bytes 93323264 | tf_op jit(solution)/shard_map/dot_general | solution.py:99
  508.1 46.3 %multiply_convert_fusion.1.clone.5 = bf16[512,7168]{1,0:T(8,128)(2,1)} fusion(f32[512,7168]{1,0:T(8,128)} %fusion.82, bf16[512,5120]{1,0:T(8,128)(2,1)S(1)} %copy-done.23, bf16[2,5120,7168]{2,1,0:T(8,128)(2,1)} %param.22), kind=kOutput, calls=%fused_computation.75.clone.clone.clone.2 | convolution fusion | flops 37602983936 | bytes 100663296 | tf_op jit(solution)/shard_map/dot_general | solution.py:100
  554.4 47.7 %fusion.78 = f32[512,5120]{1,0:T(8,128)} fusion(bf16[2,7168,5120]{2,1,0:T(8,128)(2,1)} %param.23, bf16[512,7168]{1,0:T(8,128)(2,1)} %multiply_convert_fusion.1.clone.5), kind=kOutput, calls=%fused_computation.56 | convolution fusion | flops 37580963840 | bytes 91226112 | tf_op jit(solution)/shard_map/dot_general | solution.py:102
  602.1 119.2 %reduce-scatter.7.cloned.1.call-done = f32[256,5120]{1,0:T(8,128)} async-done(((f32[512,5120]{1,0:T(8,128)}), f32[256,5120]{1,0:T(8,128)}) %reduce-scatter.7.cloned.1.call-update) | async-done | bytes 5242896 | tf_op jit(solution)/shard_map/reduce_scatter | solution.py:103
  736.7 58.3 %all-gather.17.cloned.1.call-done = bf16[512,5120]{1,0:T(8,128)(2,1)} async-done(((bf16[256,5120]{1,0:T(8,128)(2,1)}), bf16[512,5120]{1,0:T(8,128)(2,1)}) %all-gather.17.cloned.1.call-update) | async-done | bytes 5242896 | tf_op jit(solution)/shard_map/all_gather | solution.py:75
  802.6 27.6 %copy.68 = bf16[1,5120,16,128]{1,3,2,0:T(8,128)(2,1)} copy(bf16[1,5120,16,128]{3,2,1,0:T(8,128)(2,1)} %get-tuple-element.243) | data formatting | bytes 41943040
  838.3 16.1 %fusion.152 = f32[512,2048]{0,1:S(1)} fusion(bf16[512,5120]{1,0:T(8,128)(2,1)} %all-gather.17.cloned.1.call-done, bf16[5120,2048]{0,1:T(8,128)(2,1)} %bitcast.301), kind=kOutput, calls=%fused_computation.161 | convolution fusion | flops 10737418240 | bytes 30408704
  873.3 60.8 %while.23 = (s32[]{:T(128)}, bf16[4,128,4,4,128]{4,1,0,3,2:T(8,128)(2,1)}, s32[4,128]{1,0:T(4,128)}, bf16[4,128,4,4,128]{4,1,3,2,0:T(8,128)(2,1)}, bf16[2048,4,1...) while((s32[]{:T(128)}, ...), condition=%wide.region_12.13_spmd.clone, body=%wide.region_9.12_spmd.clone.sunk | while | flops 2194409472 | bytes 65089484 | solution.py:48
  934.0 17.1 %fusion.107 = f32[512,5120]{1,0:T(8,128)} fusion(bf16[512,16,128]{2,0,1:T(8,128)(2,1)} %bitcast.28, bf16[2,16,128,5120]{3,2,1,0:T(8,128)(2,1)} %param.20), kind=kOutput, calls=%fused_computation.77 | convolution fusion | flops 10737418240 | bytes 33554432 | tf_op jit(solution)/shard_map/rhe,hed->rd/dot_general | solution.py:95
  951.2 119.2 %reduce-scatter.9.cloned.1.call-done = f32[256,5120]{1,0:T(8,128)} async-done(((f32[512,5120]{1,0:T(8,128)}), f32[256,5120]{1,0:T(8,128)}) %reduce-scatter.9.cloned.1.call-update) | async-done | bytes 5242896 | tf_op jit(solution)/shard_map/reduce_scatter | solution.py:96
  1077.7 66.3 %all-gather.23.cloned.1.call-done = bf16[512,5120]{1,0:T(8,128)(2,1)} async-done(((bf16[256,5120]{1,0:T(8,128)(2,1)}), bf16[512,5120]{1,0:T(8,128)(2,1)}) %all-gather.23.cloned.1.call-update) | async-done | bytes 5242896 | tf_op jit(solution)/shard_map/all_gather | solution.py:98
  1144.1 48.7 %fusion.76 = f32[512,7168]{1,0:T(8,128)} fusion(bf16[512,5120]{1,0:T(8,128)(2,1)} %all-gather.23.cloned.1.call-done, bf16[2,5120,7168]{2,1,0:T(8,128)(2,1)} %param.21), kind=kOutput, calls=%fused_computation.54 | convolution fusion | flops 37580963840 | bytes 93323264 | tf_op jit(solution)/shard_map/dot_general | solution.py:99
  1192.8 46.2 %multiply_convert_fusion.clone.5 = bf16[512,7168]{1,0:T(8,128)(2,1)} fusion(f32[512,7168]{1,0:T(8,128)} %fusion.76, bf16[512,5120]{1,0:T(8,128)(2,1)S(1)} %copy-done.24, bf16[2,5120,7168]{2,1,0:T(8,128)(2,1)} %param.22), kind=kOutput, calls=%fused_computation.74.clone.clone.clone.2 | convolution fusion | flops 37602983936 | bytes 100663296 | tf_op jit(solution)/shard_map/dot_general | solution.py:100
  1239.0 47.8 %fusion.72 = f32[512,5120]{1,0:T(8,128)} fusion(bf16[2,7168,5120]{2,1,0:T(8,128)(2,1)} %param.23, bf16[512,7168]{1,0:T(8,128)(2,1)} %multiply_convert_fusion.clone.5), kind=kOutput, calls=%fused_computation.50 | convolution fusion | flops 37580963840 | bytes 91226112 | tf_op jit(solution)/shard_map/dot_general | solution.py:102
  1286.9 119.2 %reduce-scatter.11.cloned.1.call-done = f32[256,5120]{1,0:T(8,128)} async-done(((f32[512,5120]{1,0:T(8,128)}), f32[256,5120]{1,0:T(8,128)}) %reduce-scatter.11.cloned.1.call-update) | async-done | bytes 5242896 | tf_op jit(solution)/shard_map/reduce_scatter | solution.py:103
  (212 shorter events, 240.5 us)
Async XLA Ops:
  6.5 77.0 %all-gather.9.cloned.1.call-start = ((), (), s32[]{:S(2)}) async-start(), calls=%async_computation.4 | async-start | bytes 7864320 | tf_op jit(solution)/shard_map/all_gather | solution.py:75
  14.3 171.6 %all-gather.11.cloned.1.call-start = ((), (), s32[]{:S(2)}) async-start(), calls=%async_computation.5 | async-start | bytes 2621440 | tf_op jit(solution)/shard_map/all_gather | solution.py:91
  31.8 140.2 %copy-start.7 = (f32[512,64]{0,1:T(8,128)}, f32[512,64]{0,1:T(8,128)S(1)}, u32[]{:S(2)}) copy-start(f32[512,64]{0,1:T(8,128)S(1)} %get-tuple-element.259) | copy-start | bytes 393220
  31.8 140.2 %copy-start.9 = (f32[512,64]{0,1:T(8,128)}, f32[512,64]{0,1:T(8,128)S(1)}, u32[]{:S(2)}) copy-start(f32[512,64]{0,1:T(8,128)S(1)} %get-tuple-element.260) | copy-start | bytes 393220
  91.1 97.9 %all-gather.13.cloned.1.call-start = ((), (), s32[]{:S(2)}) async-start(), calls=%async_computation.6 | async-start | bytes 2621440 | tf_op jit(solution)/shard_map/all_gather | solution.py:92
  156.0 229.4 %reduce-scatter.5.cloned.1.call-start = ((), (), s32[]{:S(2)}) async-start(), calls=%async_computation.7 | async-start | bytes 15728640 | tf_op jit(solution)/shard_map/reduce_scatter | solution.py:96
  248.8 17.4 %copy-start.20 = (pred[256]{0:T(512)(128)(4,1)}, pred[256]{0:T(512)(128)(4,1)S(1)}, u32[]{:S(2)}) copy-start(pred[256]{0:T(512)(128)(4,1)S(1)} %get-tuple-element.506) | copy-start | bytes 772
  248.8 17.4 %copy-start.22 = (s32[4,128]{1,0:T(4,128)}, s32[4,128]{1,0:T(4,128)S(1)}, u32[]{:S(2)}) copy-start(s32[4,128]{1,0:T(4,128)S(1)} %get-tuple-element.507) | copy-start | bytes 6148
  266.2 119.3 %copy-start.2 = (bf16[256,5120]{1,0:T(8,128)(2,1)S(1)}, bf16[256,5120]{1,0:T(8,128)(2,1)}, u32[]{:S(2)}) copy-start(bf16[256,5120]{1,0:T(8,128)(2,1)} %param.14) | copy-start | bytes 7864324
  266.2 192.9 %all-gather.15.cloned.1.call-start = ((), (), s32[]{:S(2)}) async-start(), calls=%async_computation.8 | async-start | bytes 7864320 | tf_op jit(solution)/shard_map/all_gather | solution.py:98
  392.8 328.5 %reduce-scatter.7.cloned.1.call-start = ((), (), s32[]{:S(2)}) async-start(), calls=%async_computation.9 | async-start | bytes 15728640 | tf_op jit(solution)/shard_map/reduce_scatter | solution.py:103
  459.1 49.0 %copy-start.23 = (bf16[512,5120]{1,0:T(8,128)(2,1)S(1)}, bf16[512,5120]{1,0:T(8,128)(2,1)}, u32[]{:S(2)}) copy-start(bf16[512,5120]{1,0:T(8,128)(2,1)} %all-gather.15.cloned.1.call-done) | copy-start | bytes 15728644
  602.0 119.2 %copy-start.6 = (bf16[256,5120]{1,0:T(8,128)(2,1)S(1)}, bf16[256,5120]{1,0:T(8,128)(2,1)}, u32[]{:S(2)}) copy-start(bf16[256,5120]{1,0:T(8,128)(2,1)} %copy-done.5) | copy-start | bytes 7864324
  602.1 124.3 %copy-start.17 = (f32[1,5120]{1,0:T(1,128)S(1)}, f32[1,5120]{1,0:T(1,128)}, u32[]{:S(2)}) copy-start(f32[1,5120]{1,0:T(1,128)} %get-tuple-element.257) | copy-start | bytes 61444
  602.1 192.9 %all-gather.17.cloned.1.call-start = ((), (), s32[]{:S(2)}) async-start(), calls=%async_computation.10 | async-start | bytes 7864320 | tf_op jit(solution)/shard_map/all_gather | solution.py:75
  728.7 139.7 %all-gather.19.cloned.1.call-start = ((), (), s32[]{:S(2)}) async-start(), calls=%async_computation.11 | async-start | bytes 2621440 | tf_op jit(solution)/shard_map/all_gather | solution.py:91
  802.6 68.9 %all-gather.21.cloned.1.call-start = ((), (), s32[]{:S(2)}) async-start(), calls=%async_computation.12 | async-start | bytes 2621440 | tf_op jit(solution)/shard_map/all_gather | solution.py:92
  838.3 232.1 %reduce-scatter.9.cloned.1.call-start = ((), (), s32[]{:S(2)}) async-start(), calls=%async_computation.13 | async-start | bytes 15728640 | tf_op jit(solution)/shard_map/reduce_scatter | solution.py:96
  951.1 119.2 %copy-start.4 = (bf16[256,5120]{1,0:T(8,128)(2,1)S(1)}, bf16[256,5120]{1,0:T(8,128)(2,1)}, u32[]{:S(2)}) copy-start(bf16[256,5120]{1,0:T(8,128)(2,1)} %copy-done.3) | copy-start | bytes 7864324
  951.2 124.3 %copy-start.18 = (f32[1,5120]{1,0:T(1,128)S(1)}, f32[1,5120]{1,0:T(1,128)}, u32[]{:S(2)}) copy-start(f32[1,5120]{1,0:T(1,128)} %get-tuple-element.255) | copy-start | bytes 61444
  951.2 192.9 %all-gather.23.cloned.1.call-start = ((), (), s32[]{:S(2)}) async-start(), calls=%async_computation.14 | async-start | bytes 7864320 | tf_op jit(solution)/shard_map/all_gather | solution.py:98
  1077.7 328.4 %reduce-scatter.11.cloned.1.call-start = ((), (), s32[]{:S(2)}) async-start(), calls=%async_computation.15 | async-start | bytes 15728640 | tf_op jit(solution)/shard_map/reduce_scatter | solution.py:103
  1144.1 48.7 %copy-start.24 = (bf16[512,5120]{1,0:T(8,128)(2,1)S(1)}, bf16[512,5120]{1,0:T(8,128)(2,1)}, u32[]{:S(2)}) copy-start(bf16[512,5120]{1,0:T(8,128)(2,1)} %all-gather.23.cloned.1.call-done) | copy-start | bytes 15728644
  1286.8 119.2 %copy-start.1 = (bf16[256,5120]{1,0:T(8,128)(2,1)S(1)}, bf16[256,5120]{1,0:T(8,128)(2,1)}, u32[]{:S(2)}) copy-start(bf16[256,5120]{1,0:T(8,128)(2,1)} %copy-done) | copy-start | bytes 7864324
  (21 other events, 141.4 us)
Sparse Core Ops, SparseCore 0:
  14.5 69.0 all-gather.8
  91.2 19.5 all-gather.10
  156.1 19.5 all-gather.12
  266.4 119.0 reduce-scatter.4
  392.9 66.1 all-gather.14
  602.2 119.0 reduce-scatter.6
  728.8 66.1 all-gather.16
  802.7 19.5 all-gather.18
  838.4 19.5 all-gather.20
  951.3 119.0 reduce-scatter.8
  1077.8 66.2 all-gather.22
  1287.0 119.0 reduce-scatter.10
where the time goes:
time: 1430 us; the launch traced here: 1420 us
  waiting for transfers between devices  718 us (50%)
  matrix products  457 us (32%)
  local copies, waits for them, and re-layouts  147 us (10%)
  other arithmetic  80.3 us (6%)
    reduce_scatter x2, waiting for transfers between devices, body(): mlp_out = lax.psum_scatter(mlp_part, 'tp', scatter_dimension=0, tiled=True)  238 us
    reduce_scatter x2, waiting for transfers between devices, body(): lax.psum_scatter(attn_part, 'tp', scatter_dimension=0, tiled=True)  237 us
    all_gather x2, waiting for transfers between devices, body(): lax.all_gather(rms_norm(hidden_mid, norm_mlp[layer_idx]), 'tp', axis=0, t...  133 us
    all_gather x2, waiting for transfers between devices, body(): lax.all_gather(rms_norm(hidden, norm_attn[layer_idx]), 'tp', axis=0, tile...  110 us
    dot_general x2, matrix products, body(): jnp.dot(normed_mlp, w_gate[layer_idx], preferred_element_type=jnp.float32)  97.7 us
    dot_general x2, matrix products, body(): jnp.dot(hidden_act, w_down[layer_idx], preferred_element_type=jnp.float32)  95.5 us
    dot_general x2, matrix products, body(): jnp.dot(normed_mlp, w_up[layer_idx], preferred_element_type=jnp.float32)  92.5 us
    unnamed x55, local copies, waits for them, and re-layouts  66.5 us
  transfers between devices with their start and end apart: 12, of which 8 were waited for; matrix products, arithmetic and copies ran while one was open for 14% of the time, Pallas kernels for 0%

commit v1 on v0

v1 whole, which is shorter than its diff:
```python
import functools
import math
import jax
import jax.numpy as jnp
from jax import lax
from jax.experimental import pallas as pl
from jax.experimental.pallas import tpu as pltpu
from jax.sharding import PartitionSpec as P

F32 = jnp.float32
BF16 = jnp.bfloat16
VMEM_LIMIT = 56 * 1024 * 1024


def rms_norm(hidden, gain):
    hidden_f = hidden.astype(F32)
    inv_rms = lax.rsqrt(jnp.mean(hidden_f * hidden_f, axis=-1, keepdims=True) + 1e-5)
    return (hidden_f * inv_rms * gain.astype(F32)).astype(BF16)


def resident(shape):
    return pl.BlockSpec(shape, lambda j: (0,) * len(shape), pipeline_mode=pl.Buffered(1))


def gate_up_kernel(a_ref, b_ref, wg_ref, wu_ref, o_ref, x_ref):
    seg = a_ref.shape[0]

    @pl.when(pl.program_id(0) == 0)
    def _():
        x_ref[:seg] = a_ref[...]
        x_ref[seg:] = b_ref[...]

    gate = jnp.dot(x_ref[...], wg_ref[...], preferred_element_type=F32)
    up = jnp.dot(x_ref[...], wu_ref[...], preferred_element_type=F32)
    o_ref[...] = (jax.nn.silu(gate) * up).astype(BF16)


def gate_up(own, peer, w_gate, w_up, li, tile=512):
    seg, d = own.shape
    n = w_gate.shape[2]
    wspec = pl.BlockSpec((None, d, tile), lambda j: (li, 0, j))
    return pl.pallas_call(
        gate_up_kernel,
        out_shape=jax.ShapeDtypeStruct((2 * seg, n), BF16),
        grid=(n // tile,),
        in_specs=[resident((seg, d)), resident((seg, d)), wspec, wspec],
        out_specs=pl.BlockSpec((2 * seg, tile), lambda j: (0, j)),
        scratch_shapes=[pltpu.VMEM((2 * seg, d), BF16)],
        compiler_params=pltpu.CompilerParams(vmem_limit_bytes=VMEM_LIMIT),
        cost_estimate=pl.CostEstimate(flops=8 * seg * d * n, bytes_accessed=4 * d * n, transcendentals=2 * seg * n),
    )(own, peer, w_gate, w_up)


def split_kernel(x_ref, w_ref, own_ref, send_ref):
    seg = own_ref.shape[0]
    part = jnp.dot(x_ref[...], w_ref[...], preferred_element_type=F32)
    own_ref[...] = part[:seg]
    send_ref[...] = part[seg:]


def split_proj(x, w, li, tile=512, first=0, count=None):
    rows, k = x.shape
    seg = rows // 2
    n = w.shape[2] if count is None else count
    base = first // tile
    return pl.pallas_call(
        split_kernel,
        out_shape=[jax.ShapeDtypeStruct((seg, n), F32)] * 2,
        grid=(n // tile,),
        in_specs=[resident((rows, k)), pl.BlockSpec((None, k, tile), lambda j: (li, 0, base + j))],
        out_specs=[pl.BlockSpec((seg, tile), lambda j: (0, j))] * 2,
        compiler_params=pltpu.CompilerParams(vmem_limit_bytes=VMEM_LIMIT),
        cost_estimate=pl.CostEstimate(flops=2 * rows * k * n, bytes_accessed=2 * k * n + 4 * rows * n, transcendentals=0),
    )(x, w)


def rotate(x, cos, sin):
    return x * cos + pltpu.roll(x, x.shape[1] // 2, axis=1) * sin


def kv_kernel(a_ref, b_ref, wk_ref, wv_ref, cos_ref, sin_ref, o_ref, x_ref):
    seg = a_ref.shape[0]
    head = cos_ref.shape[1]
    tile = wk_ref.shape[1]
    step = pl.program_id(0)
    width = o_ref.shape[1] // 2

    @pl.when(step == 0)
    def _():
        x_ref[:seg] = a_ref[...]
        x_ref[seg:] = b_ref[...]

    x = x_ref[...]
    k = jnp.dot(x, wk_ref[...], preferred_element_type=F32)
    base = pl.multiple_of(step * tile, tile)
    rot = [rotate(k[:, h:h + head], cos_ref[...], sin_ref[...]).astype(BF16) for h in range(0, tile, head)]
    o_ref[:, pl.ds(base, tile)] = jnp.concatenate(rot, axis=1)
    o_ref[:, pl.ds(width + base, tile)] = jnp.dot(x, wv_ref[...], preferred_element_type=F32).astype(BF16)


def kv_proj(own, peer, w_k, w_v, cos, sin, li, tile=256):
    seg, d = own.shape
    n = w_k.shape[2]
    head = cos.shape[1]
    wspec = pl.BlockSpec((None, d, tile), lambda j: (li, 0, j))
    return pl.pallas_call(
        kv_kernel,
        out_shape=jax.ShapeDtypeStruct((2 * seg, 2 * n), BF16),
        grid=(n // tile,),
        in_specs=[resident((seg, d)), resident((seg, d)), wspec, wspec, resident((2 * seg, head)), resident((2 * seg, head))],
        out_specs=pl.BlockSpec((2 * seg, 2 * n), lambda j: (0, 0)),
        scratch_shapes=[pltpu.VMEM((2 * seg, d), BF16)],
        compiler_params=pltpu.CompilerParams(vmem_limit_bytes=VMEM_LIMIT),
        cost_estimate=pl.CostEstimate(flops=8 * seg * d * n, bytes_accessed=4 * d * n, transcendentals=0),
    )(own, peer, w_k, w_v, cos, sin)


def attn_kernel(seg_q_ref, seg_k_ref, q_ref, cos_ref, sin_ref, *rest, seg, group, head_dim, free, parts):
    total = free + parts
    k_refs = rest[0:2 * total:2]
    v_refs = rest[1:2 * total:2]
    o_ref, s_ref, qs_ref, m_ref, l_ref, acc_ref = rest[2 * total:]
    rate = math.log2(math.e) / math.sqrt(head_dim)
    n_q = q_ref.shape[0] // seg
    rows = group * seg
    q_row = lax.broadcasted_iota(jnp.int32, (seg, seg), 0)
    k_col = lax.broadcasted_iota(jnp.int32, (seg, seg), 1)

    def scores(i, p):
        return lax.dot_general(qs_ref[i], k_refs[p][...], (((1,), (1,)), ((), ())), preferred_element_type=F32)

    def weigh(i, p):
        top = m_ref[i]
        w0 = jnp.exp2((s_ref[i, p, :, :seg] - top) * rate)
        w1 = jnp.exp2((s_ref[i, p, :, seg:] - top) * rate)
        w = jnp.concatenate([w0.astype(BF16), w1.astype(BF16)], axis=1)
        return w0 + w1, jnp.dot(w, v_refs[p][...], preferred_element_type=F32)

    for i in range(n_q):
        cos = cos_ref[i * seg:(i + 1) * seg]
        sin = sin_ref[i * seg:(i + 1) * seg]
        for g in range(group):
            q = q_ref[i * seg:(i + 1) * seg, g * head_dim:(g + 1) * head_dim]
            qs_ref[i, g * seg:(g + 1) * seg, :] = rotate(q, cos, sin).astype(BF16)
        top = jnp.full((rows, seg), -jnp.inf, F32)
        for p in range(free):
            s = scores(i, p)
            s_ref[i, p] = s
            top = jnp.maximum(top, jnp.maximum(s[:, :seg], s[:, seg:]))
        m_ref[i] = top
    seen = {}
    for i in range(n_q):
        sq = seg_q_ref[i]
        for p in range(free, total):
            sk0 = seg_k_ref[2 * (p - free)]
            sk1 = seg_k_ref[2 * (p - free) + 1]
            seen[i, p] = jnp.minimum(sk0, sk1) <= sq

            @pl.when(seen[i, p])
            def _(i=i, p=p, sk0=sk0, sk1=sk1, sq=sq):
                s = scores(i, p)
                top = m_ref[i]
                for b, sk in enumerate((sk0, sk1)):
                    bias = jnp.where(k_col <= q_row + (sq - sk) * seg, 0.0, -jnp.inf)
                    sb = s[:, b * seg:(b + 1) * seg] + jnp.concatenate([bias] * group, axis=0)
                    s_ref[i, p, :, b * seg:(b + 1) * seg] = sb
                    top = jnp.maximum(top, sb)
                m_ref[i] = top

    for i in range(n_q):
        m_ref[i] = jnp.broadcast_to(jnp.max(m_ref[i], axis=-1, keepdims=True), (rows, seg))
        lsum = jnp.zeros((rows, seg), F32)
        acc = jnp.zeros((rows, head_dim), F32)
        for p in range(free):
            wl, wa = weigh(i, p)
            lsum = lsum + wl
            acc = acc + wa
        l_ref[i] = lsum
        acc_ref[i] = acc
    for i in range(n_q):
        for p in range(free, total):
            @pl.when(seen[i, p])
            def _(i=i, p=p):
                wl, wa = weigh(i, p)
                l_ref[i] += wl
                acc_ref[i] += wa

    for i in range(n_q):
        out = acc_ref[i] / jnp.sum(l_ref[i], axis=-1, keepdims=True)
        for g in range(group):
            o_ref[i * seg:(i + 1) * seg, g * head_dim:(g + 1) * head_dim] = out[g * seg:(g + 1) * seg, :].astype(BF16)


def attend(q_raw, cos, sin, free_parts, kv_parts, seg_q, seg_k, seg, group, head_dim):
    rows = q_raw.shape[0]
    n_q = rows // seg
    width = group * head_dim
    kv_loc = q_raw.shape[1] // width
    every = list(free_parts) + list(kv_parts)
    total = len(every)
    k_spec = pl.BlockSpec((2 * seg, head_dim), lambda h, *_: (0, h))
    v_spec = pl.BlockSpec((2 * seg, head_dim), lambda h, *_: (0, kv_loc + h))
    t_spec = pl.BlockSpec((rows, head_dim), lambda h, *_: (0, 0))
    q_spec = pl.BlockSpec((rows, width), lambda h, *_: (0, h))
    keys = total * 2 * seg
    return pl.pallas_call(
        functools.partial(attn_kernel, seg=seg, group=group, head_dim=head_dim, free=len(free_parts), parts=len(kv_parts)),
        out_shape=jax.ShapeDtypeStruct((rows, kv_loc * width), BF16),
        grid_spec=pltpu.PrefetchScalarGridSpec(
            num_scalar_prefetch=2,
            grid=(kv_loc,),
            in_specs=[q_spec, t_spec, t_spec] + [k_spec, v_spec] * total,
            out_specs=q_spec,
            scratch_shapes=[
                pltpu.VMEM((n_q, total, group * seg, 2 * seg), F32),
                pltpu.VMEM((n_q, group * seg, head_dim), BF16),
                pltpu.VMEM((n_q, group * seg, seg), F32),
                pltpu.VMEM((n_q, group * seg, seg), F32),
                pltpu.VMEM((n_q, group * seg, head_dim), F32),
            ],
        ),
        compiler_params=pltpu.CompilerParams(vmem_limit_bytes=32 * 1024 * 1024),
        cost_estimate=pl.CostEstimate(
            flops=4 * rows * keys * kv_loc * width,
            bytes_accessed=rows * kv_loc * width * 6 + keys * kv_loc * head_dim * 4,
            transcendentals=rows * keys * kv_loc * group,
        ),
    )(seg_q, seg_k, q_raw, cos, sin, *[v for part in every for v in (part, part)])


def solution(mesh):
    tp_size = mesh.shape['tp']
    cp_size = mesh.shape['cp']
    dev_total = tp_size * cp_size
    row_spec = P(('dp', 'tp', 'cp'), None)
    gain_spec = P(None, None)
    q_spec = P(None, None, 'tp', None)
    col_spec = P(None, None, 'tp')
    o_spec = P(None, 'tp', None, None)
    down_spec = P(None, 'tp', None)
    swap = [(0, 1), (1, 0)]

    def body(tokens, norm_attn, norm_mlp, w_q, w_k, w_v, w_o, w_gate, w_up, w_down):
        layers = w_q.shape[0]
        d_model = tokens.shape[1]
        heads_loc = w_q.shape[2]
        head_dim = w_q.shape[3]
        kv_cols = w_k.shape[2]
        kv_loc = kv_cols // head_dim
        group = heads_loc // kv_loc
        half = head_dim // 2
        seg = tokens.shape[0] // 2
        tp_idx = lax.axis_index('tp')
        cp_idx = lax.axis_index('cp')
        tps = jnp.stack([tp_idx, 1 - tp_idx])
        cps = jnp.stack([cp_idx, cp_idx ^ 1, cp_idx ^ 2, cp_idx ^ 3])
        dev_q = tps * cp_size + cp_idx
        dev_k = jnp.stack([tps * cp_size + cps[0], tps * cp_size + cps[1], tps * cp_size + cps[2], tps * cp_size + cps[3]]).reshape(-1)
        seg_q = [dev_q, 2 * dev_total - 1 - dev_q]
        seg_k = [dev_k, 2 * dev_total - 1 - dev_k]
        inv_freq = 500000.0 ** (-(jnp.arange(half, dtype=F32) * 2.0 / head_dim))
        cos, sin = [], []
        for c in range(2):
            pos = (seg_q[c][:, None] * seg + jnp.arange(seg)[None, :]).reshape(-1)
            ang = pos.astype(F32)[:, None] * inv_freq[None, :]
            c_half, s_half = jnp.cos(ang), jnp.sin(ang)
            cos.append(jnp.concatenate([c_half, c_half], axis=1))
            sin.append(jnp.concatenate([-s_half, s_half], axis=1))

        def swap_tp(v):
            return lax.ppermute(v, 'tp', swap)

        def swap_cp(v, bit):
            return lax.ppermute(v, 'cp', [(i, i ^ bit) for i in range(cp_size)])

        def after(v, *tokens_):
            return lax.optimization_barrier((v,) + tokens_)[0]

        def gather_kv(kv):
            core = swap_cp(kv, 1)
            cross = swap_cp(kv, 2)
            return [kv, core, cross, swap_cp(cross, 1)]

        def kv_of(own, peer, li, c):
            return kv_proj(own, peer, w_k, w_v, cos[c], sin[c], li)

        def q_of(own, peer, wq):
            nn = jnp.concatenate([own, peer], axis=0)
            return jnp.einsum('rd,dhe->rhe', nn, wq, preferred_element_type=F32).reshape(2 * seg, heads_loc * head_dim)

        def mix_a(q, parts):
            return attend(q, cos[0], sin[0], [], parts, seg_q[0], seg_k[0], seg, group, head_dim)

        def mix_b(q, parts_a, parts_b):
            return attend(q, cos[1], sin[1], parts_a, parts_b, seg_q[1], seg_k[1], seg, group, head_dim)

        def add(base, part, other):
            return (base.astype(F32) + (part + other)).astype(BF16)

        wo = w_o.reshape(layers, heads_loc * head_dim, d_model)
        xa, xb = tokens[:seg], tokens[seg:]
        na = rms_norm(xa, norm_attn[0])
        nb = rms_norm(xb, norm_attn[0])
        nap, nbp = swap_tp(na), swap_tp(nb)
        wq = after(w_q, na, nb)[0]
        for li in range(layers):
            kva = kv_of(na if li else after(na, wq), nap, li, 0)
            parts_a = gather_kv(kva)
            qa = q_of(na, after(nap, kva), wq)
            if li > 0:
                ma = mix_a(qa, parts_a)
                pa, sa = split_proj(ma, wo, li, 2560)
                xb = add(hb, down_b, after(rb, pa))
                nb = rms_norm(xb, norm_attn[li])
                nbp = swap_tp(nb)
                ra = swap_tp(after(sa, nb))
                kvb = kv_of(nb, nbp, li, 1)
                parts_b = gather_kv(kvb)
                qb = q_of(nb, after(nbp, kvb), wq)
            else:
                kvb = kv_of(after(nb, qa), nbp, li, 1)
                parts_b = gather_kv(kvb)
                qb = q_of(nb, after(nbp, kvb), wq)
                ma = mix_a(after(qa, qb), parts_a)
                pa, sa = split_proj(ma, wo, li, 2560)
                ra = swap_tp(sa)
            mb = mix_b(after(qb, pa), parts_a, parts_b)
            pb, sb = split_proj(mb, wo, li, 2560)
            ha = add(xa, pa, after(ra, pb))
            na = rms_norm(ha, norm_mlp[li])
            nap = swap_tp(na)
            rb = swap_tp(after(sb, na))
            if li + 1 < layers:
                wq = after(w_q, na)[li + 1]
                na = after(na, wq)
            act_a = gate_up(na, nap, w_gate, w_up, li)
            hb = add(xb, pb, after(rb, act_a))
            nb = rms_norm(hb, norm_mlp[li])
            nbp = swap_tp(nb)
            down_a, sa = split_proj(after(act_a, nb), w_down, li)
            ra = swap_tp(sa)
            act_b = gate_up(after(nb, down_a), nbp, w_gate, w_up, li)
            xa = add(ha, down_a, after(ra, act_b))
            if li + 1 < layers:
                na = rms_norm(xa, norm_attn[li + 1])
                nap = swap_tp(na)
            down_b, sb = split_proj(after(act_b, xa), w_down, li)
            rb = swap_tp(sb)
        xb = add(hb, down_b, rb)
        return jnp.concatenate([xa, xb], axis=0)

    return jax.shard_map(
        body,
        mesh=mesh,
        in_specs=(row_spec, gain_spec, gain_spec, q_spec, col_spec, col_spec, o_spec, col_spec, col_spec, down_spec),
        out_specs=row_spec,
        check_vma=False,
    )
```

time: 1430 us -> 893 us (0.62)
  Pallas kernels: 0 us -> 501 us
  waiting for transfers between devices: 718 us -> 236 us
  matrix products: 457 us -> 42.5 us
  local copies, waits for them, and re-layouts: 147 us -> 45.8 us
  other arithmetic: 80.3 us -> 29.4 us
  starting transfers between devices: 0.64 us -> 27.4 us
    pallas_call x0 -> x20, Pallas kernels: none -> 501 us  [the longest x4 220 us: gate_up(): pl.pallas_call(gate_up_kernel, out_shape=jax.ShapeDtypeStruct((2 * seg, n...]
    reduce_scatter x4 -> x0, waiting for transfers between devices: 475 us -> none  [the longest x2 238 us: body(): mlp_out = lax.psum_scatter(mlp_part, 'tp', scatter_dimension=0, tiled=True)]
    dot_general x28 -> x4, matrix products: 425 us -> 42.5 us  [q_of(): jnp.einsum('rd,dhe->rhe', nn, wq, preferred_element_type=F32)]
    all_gather x8 -> x0, waiting for transfers between devices: 243 us -> none  [the longest x2 133 us: body(): lax.all_gather(rms_norm(hidden_mid, norm_mlp[layer_idx]), 'tp', axis=0, t...]
    ppermute x0 -> x28, waiting for transfers between devices: none -> 236 us  [the longest x16 225 us: swap_tp(): return lax.ppermute(v, 'tp', swap)]
    unnamed x55 -> x104, local copies, waits for them, and re-layouts: 66.5 us -> 9.53 us
    reduce_sum x8 -> x0, other arithmetic: 35.2 us -> none  [one_block(): row_sum = jnp.sum(weights, axis=-1, keepdims=True)]
    unnamed x2 -> x0, matrix products: 31.9 us -> none
  transfers between devices with their start and end apart: 12 -> 28, of which waited for: 8 -> 12; matrix products, arithmetic and copies ran while one was open for 14% -> 9% of each run, Pallas kernels for 0% -> 51%
where the time goes in v1:
time: 893 us; the launch traced here: 883 us
  Pallas kernels  501 us (56%)
  waiting for transfers between devices  236 us (26%)
  local copies, waits for them, and re-layouts  45.8 us (5%)
  matrix products  42.5 us (5%)
  other arithmetic  29.4 us (3%)
  starting transfers between devices  27.4 us (3%)
    ppermute x16, waiting for transfers between devices, swap_tp(): return lax.ppermute(v, 'tp', swap)  225 us
    pallas_call x4, Pallas kernels, gate_up(): pl.pallas_call(gate_up_kernel, out_shape=jax.ShapeDtypeStruct((2 * seg, n...  220 us
    pallas_call x8, Pallas kernels, split_proj(): pl.pallas_call(split_kernel, out_shape=[jax.ShapeDtypeStruct((seg, n), F3...  174 us
    pallas_call x4, Pallas kernels, attend(): pl.pallas_call(functools.partial(attn_kernel, seg=seg, group=group, head_...  76.5 us
    dot_general x4, matrix products, q_of(): jnp.einsum('rd,dhe->rhe', nn, wq, preferred_element_type=F32)  42.5 us
    pallas_call x4, Pallas kernels, kv_proj(): pl.pallas_call(kv_kernel, out_shape=jax.ShapeDtypeStruct((2 * seg, 2 * n)...  30.1 us
    slice x1, local copies, waits for them, and re-layouts, body(): wq = after(w_q, na)[li + 1]  18.2 us
    slice x1, local copies, waits for them, and re-layouts, body(): wq = after(w_q, na, nb)[0]  18.1 us
  transfers between devices with their start and end apart: 28, of which 12 were waited for; matrix products, arithmetic and copies ran while one was open for 9% of the time, Pallas kernels for 51%

profile of v1, /device:TPU:0, one launch (start us, length us, event | category | flops | bytes accessed | tf_op | source)
XLA Modules:
  0.0 882.9 jit_solution(14039085617241247524)
XLA Ops:
  8.4 18.1 %slice.31 = bf16[1,5120,16,128]{3,2,1,0:T(8,128)(2,1)} slice(bf16[2,5120,16,128]{3,2,1,0:T(8,128)(2,1)} %param.13), slice={[0:1], [0:5120], [0:16], [0:128]} | slice | bytes 41943040 | tf_op jit(solution)/shard_map/slice | solution.py:305
  29.3 35.7 %collective-permute-done.b_ref = bf16[128,5120]{1,0:T(8,128)(2,1)} collective-permute-done((bf16[128,5120]{1,0:T(8,128)(2,1)S(1)}, bf16[128,5120]{1,0:T(8,128)(2,1)}, u32[]{:S(2)}, u32[]{:S(2)}) %collective-permute-start) | collective-permute-done | bytes 1310752 | tf_op jit(solution)/shard_map/ppermute | solution.py:271
  104.1 13.8 %shard_map.102.x_ref = bf16[256,2048]{1,0:T(8,128)(2,1)S(1)} custom-call(s32[2]{0:T(128)S(1)} %get-tuple-element.108.seg_q_ref, s32[8]{0:T(128)S(1)} %reshape.240.seg_k_ref, f32[256,2048]{1,0:T(8,128)S(1)} %fusion.6.q_ref, f32[256,128]{1,0:T(8,128)S(1)} %copy-done.4, f32[256,128]{1,0:T(8,128)S(1)} %copy-done.6, bf16[256,1024]{1,0:T(8,128)(2,1)S(1)} %copy-done.13, ...), custom_call_target="tpu_custom_call" | custom-call | flops 2147483648 | bytes 5242880 | tf_op jit(solution)/shard_map/pallas_call | solution.py:206
  118.9 11.8 %shard_map.103 = (f32[128,5120]{1,0:T(8,128)}, f32[128,5120]{1,0:T(8,128)}) custom-call(bf16[256,2048]{1,0:T(8,128)(2,1)} %copy-done.11, bf16[2,2048,5120]{2,1,0:T(8,128)(2,1)} %bitcast.35), custom_call_target="tpu_custom_call" | custom-call | flops 5368709120 | bytes 26214400 | tf_op jit(solution)/shard_map/pallas_call | solution.py:66
  136.6 24.5 %shard_map.104.x_ref = bf16[256,2048]{1,0:T(8,128)(2,1)S(1)} custom-call(s32[2]{0:T(128)S(1)} %get-tuple-element.127.seg_q_ref, s32[8]{0:T(128)S(1)} %broadcast_subtract_fusion.seg_k_ref, f32[256,2048]{1,0:T(8,128)S(1)} %copy-done.18, f32[256,128]{1,0:T(8,128)S(1)} %copy-done, f32[256,128]{1,0:T(8,128)S(1)} %copy-done.2, bf16[256,1024]{1,0:T(8,128)(2,1)S(1)} %copy-done.13, ...), custom_call_target="tpu_custom_call" | custom-call | flops 4294967296 | bytes 7340032 | tf_op jit(solution)/shard_map/pallas_call | solution.py:206
  162.1 11.7 %shard_map.105 = (f32[128,5120]{1,0:T(8,128)}, f32[128,5120]{1,0:T(8,128)}) custom-call(bf16[256,2048]{1,0:T(8,128)(2,1)} %copy-done.9, bf16[2,2048,5120]{2,1,0:T(8,128)(2,1)} %bitcast.36), custom_call_target="tpu_custom_call" | custom-call | flops 5368709120 | bytes 26214400 | tf_op jit(solution)/shard_map/pallas_call | solution.py:66
  173.8 15.5 %collective-permute-done.5 = f32[128,5120]{1,0:T(8,128)} collective-permute-done((f32[128,5120]{1,0:T(8,128)}, f32[128,5120]{1,0:T(8,128)}, u32[]{:S(2)}, u32[]{:S(2)}) %collective-permute-start.5) | collective-permute-done | bytes 2621472 | tf_op jit(solution)/shard_map/ppermute | solution.py:271
  194.4 29.6 %collective-permute-done.9.b_ref = bf16[128,5120]{1,0:T(8,128)(2,1)S(1)} collective-permute-done((bf16[128,5120]{1,0:T(8,128)(2,1)S(1)}, bf16[128,5120]{1,0:T(8,128)(2,1)S(1)}, u32[]{:S(2)}, u32[]{:S(2)}) %collective-permute-start.9) | collective-permute-done | bytes 1310752 | tf_op jit(solution)/shard_map/ppermute | solution.py:271
  225.1 55.2 %shard_map.106.x_ref = bf16[256,7168]{1,0:T(8,128)(2,1)} custom-call(bf16[128,5120]{1,0:T(8,128)(2,1)} %copy-done.31, bf16[128,5120]{1,0:T(8,128)(2,1)} %copy-done.45, bf16[2,5120,7168]{2,1,0:T(8,128)(2,1)} %wg_ref.7, bf16[2,5120,7168]{2,1,0:T(8,128)(2,1)} %wu_ref.7), custom_call_target="tpu_custom_call" | custom-call | flops 37580963840 | bytes 146800640 | tf_op jit(solution)/shard_map/pallas_call | solution.py:42
  285.5 31.9 %shard_map.107 = (f32[128,5120]{1,0:T(8,128)}, f32[128,5120]{1,0:T(8,128)}) custom-call(bf16[256,7168]{1,0:T(8,128)(2,1)} %shard_map.106.x_ref, bf16[2,7168,5120]{2,1,0:T(8,128)(2,1)} %w_ref.7), custom_call_target="tpu_custom_call" | custom-call | flops 18790481920 | bytes 78643200 | tf_op jit(solution)/shard_map/pallas_call | solution.py:66
  317.9 55.0 %shard_map.108.x_ref = bf16[256,7168]{1,0:T(8,128)(2,1)} custom-call(bf16[128,5120]{1,0:T(8,128)(2,1)} %copy-done.29, bf16[128,5120]{1,0:T(8,128)(2,1)} %collective-permute-done.12.b_ref, bf16[2,5120,7168]{2,1,0:T(8,128)(2,1)} %wg_ref.7, bf16[2,5120,7168]{2,1,0:T(8,128)(2,1)} %wu_ref.7), custom_call_target="tpu_custom_call" | custom-call | flops 37580963840 | bytes 146800640 | tf_op jit(solution)/shard_map/pallas_call | solution.py:42
  379.6 18.2 %slice.33 = bf16[1,5120,16,128]{3,2,1,0:T(8,128)(2,1)} slice(bf16[2,5120,16,128]{3,2,1,0:T(8,128)(2,1)} %param.13), slice={[1:2], [0:5120], [0:16], [0:128]} | slice | bytes 41943040 | tf_op jit(solution)/shard_map/slice | solution.py:334
  422.7 31.7 %shard_map.112 = (f32[128,5120]{1,0:T(8,128)}, f32[128,5120]{1,0:T(8,128)}) custom-call(bf16[256,7168]{1,0:T(8,128)(2,1)} %shard_map.108.x_ref, bf16[2,7168,5120]{2,1,0:T(8,128)(2,1)} %w_ref.7), custom_call_target="tpu_custom_call" | custom-call | flops 18790481920 | bytes 78643200 | tf_op jit(solution)/shard_map/pallas_call | solution.py:66
  465.8 13.6 %shard_map.110.x_ref = bf16[256,2048]{1,0:T(8,128)(2,1)S(1)} custom-call(s32[2]{0:T(128)S(1)} %copy-done.17, s32[8]{0:T(128)S(1)} %reshape.240.seg_k_ref, f32[256,2048]{1,0:T(8,128)S(1)} %fusion.2.q_ref, f32[256,128]{1,0:T(8,128)S(1)} %copy-done.5, f32[256,128]{1,0:T(8,128)S(1)} %copy-done.7, bf16[256,1024]{1,0:T(8,128)(2,1)S(1)} %copy-done.12, ...), custom_call_target="tpu_custom_call" | custom-call | flops 2147483648 | bytes 5242880 | tf_op jit(solution)/shard_map/pallas_call | solution.py:206
  480.4 11.8 %shard_map.111 = (f32[128,5120]{1,0:T(8,128)}, f32[128,5120]{1,0:T(8,128)}) custom-call(bf16[256,2048]{1,0:T(8,128)(2,1)} %copy-done.10, bf16[2,2048,5120]{2,1,0:T(8,128)(2,1)} %bitcast.37), custom_call_target="tpu_custom_call" | custom-call | flops 5368709120 | bytes 26214400 | tf_op jit(solution)/shard_map/pallas_call | solution.py:66
  492.2 18.9 %collective-permute-done.17 = f32[128,5120]{1,0:T(8,128)} collective-permute-done((f32[128,5120]{1,0:T(8,128)}, f32[128,5120]{1,0:T(8,128)}, u32[]{:S(2)}, u32[]{:S(2)}) %collective-permute-start.17) | collective-permute-done | bytes 2621472 | tf_op jit(solution)/shard_map/ppermute | solution.py:271
  515.6 27.1 %collective-permute-done.19.b_ref = bf16[128,5120]{1,0:T(8,128)(2,1)S(1)} collective-permute-done((bf16[128,5120]{1,0:T(8,128)(2,1)S(1)}, bf16[128,5120]{1,0:T(8,128)(2,1)S(1)}, u32[]{:S(2)}, u32[]{:S(2)}) %collective-permute-start.19) | collective-permute-done | bytes 1310752 | tf_op jit(solution)/shard_map/ppermute | solution.py:271
  572.4 24.6 %shard_map.114.x_ref = bf16[256,2048]{1,0:T(8,128)(2,1)S(1)} custom-call(s32[2]{0:T(128)S(1)} %get-tuple-element.127.seg_q_ref, s32[8]{0:T(128)S(1)} %broadcast_subtract_fusion.seg_k_ref, f32[256,2048]{1,0:T(8,128)S(1)} %fusion.q_ref, f32[256,128]{1,0:T(8,128)S(1)} %copy-done.1, f32[256,128]{1,0:T(8,128)S(1)} %copy-done.3, bf16[256,1024]{1,0:T(8,128)(2,1)S(1)} %copy-done.12, ...), custom_call_target="tpu_custom_call" | custom-call | flops 4294967296 | bytes 7340032 | tf_op jit(solution)/shard_map/pallas_call | solution.py:206
  615.7 29.6 %collective-permute-done.23.b_ref = bf16[128,5120]{1,0:T(8,128)(2,1)} collective-permute-done((bf16[128,5120]{1,0:T(8,128)(2,1)S(1)}, bf16[128,5120]{1,0:T(8,128)(2,1)}, u32[]{:S(2)}, u32[]{:S(2)}) %collective-permute-start.23) | collective-permute-done | bytes 1310752 | tf_op jit(solution)/shard_map/ppermute | solution.py:271
  645.3 55.0 %shard_map.116.x_ref = bf16[256,7168]{1,0:T(8,128)(2,1)} custom-call(bf16[128,5120]{1,0:T(8,128)(2,1)} %copy-done.32, bf16[128,5120]{1,0:T(8,128)(2,1)} %collective-permute-done.23.b_ref, bf16[2,5120,7168]{2,1,0:T(8,128)(2,1)} %wg_ref.7, bf16[2,5120,7168]{2,1,0:T(8,128)(2,1)} %wu_ref.7), custom_call_target="tpu_custom_call" | custom-call | flops 37580963840 | bytes 146800640 | tf_op jit(solution)/shard_map/pallas_call | solution.py:42
  703.5 31.8 %shard_map.117 = (f32[128,5120]{1,0:T(8,128)}, f32[128,5120]{1,0:T(8,128)}) custom-call(bf16[256,7168]{1,0:T(8,128)(2,1)} %shard_map.116.x_ref, bf16[2,7168,5120]{2,1,0:T(8,128)(2,1)} %w_ref.7), custom_call_target="tpu_custom_call" | custom-call | flops 18790481920 | bytes 78643200 | tf_op jit(solution)/shard_map/pallas_call | solution.py:66
  736.4 54.9 %shard_map.118.x_ref = bf16[256,7168]{1,0:T(8,128)(2,1)} custom-call(bf16[128,5120]{1,0:T(8,128)(2,1)} %copy-done.30, bf16[128,5120]{1,0:T(8,128)(2,1)} %collective-permute-done.26.b_ref, bf16[2,5120,7168]{2,1,0:T(8,128)(2,1)} %wg_ref.7, bf16[2,5120,7168]{2,1,0:T(8,128)(2,1)} %wu_ref.7), custom_call_target="tpu_custom_call" | custom-call | flops 37580963840 | bytes 146800640 | tf_op jit(solution)/shard_map/pallas_call | solution.py:42
  791.7 31.8 %shard_map.119 = (f32[128,5120]{1,0:T(8,128)}, f32[128,5120]{1,0:T(8,128)}) custom-call(bf16[256,7168]{1,0:T(8,128)(2,1)} %shard_map.118.x_ref, bf16[2,7168,5120]{2,1,0:T(8,128)(2,1)} %w_ref.7), custom_call_target="tpu_custom_call" | custom-call | flops 18790481920 | bytes 78643200 | tf_op jit(solution)/shard_map/pallas_call | solution.py:66
  824.6 54.1 %collective-permute-done.27 = f32[128,5120]{1,0:T(8,128)S(1)} collective-permute-done((f32[128,5120]{1,0:T(8,128)}, f32[128,5120]{1,0:T(8,128)S(1)}, u32[]{:S(2)}, u32[]{:S(2)}) %collective-permute-start.27) | collective-permute-done | bytes 2621472 | tf_op jit(solution)/shard_map/ppermute | solution.py:271
  (201 shorter events, 175.9 us)
Async XLA Ops:
  4.7 79.9 %collective-permute-start.1 = (bf16[128,5120]{1,0:T(8,128)(2,1)S(1)}, bf16[128,5120]{1,0:T(8,128)(2,1)}, u32[]{:S(2)}, u32[]{:S(2)}) collective-permute-start(bf16[128,5120]{1,0:T(8,128)(2,1)S(1)} %get-tuple-element.52.a_ref), channel_id=1, source_target_pairs={{0,4},{4,0},{1,5},{5,1},{2,6},{6,2},{3,7},{7,3}} | collective-permute-start | bytes 3932168 | tf_op jit(solution)/shard_map/ppermute | solution.py:271
  8.1 56.9 %collective-permute-start = (bf16[128,5120]{1,0:T(8,128)(2,1)S(1)}, bf16[128,5120]{1,0:T(8,128)(2,1)}, u32[]{:S(2)}, u32[]{:S(2)}) collective-permute-start(bf16[128,5120]{1,0:T(8,128)(2,1)S(1)} %get-tuple-element.50.a_ref), channel_id=1, source_target_pairs={{0,4},{4,0},{1,5},{5,1},{2,6},{6,2},{3,7},{7,3}} | collective-permute-start | bytes 3932168 | tf_op jit(solution)/shard_map/ppermute | solution.py:271
  72.6 20.0 %collective-permute-start.3 = (bf16[256,1024]{1,0:T(8,128)(2,1)}, bf16[256,1024]{1,0:T(8,128)(2,1)S(1)}, u32[]{:S(2)}, u32[]{:S(2)}) collective-permute-start(bf16[256,1024]{1,0:T(8,128)(2,1)} %shard_map.100.rest_0_.rest_1_), channel_id=1, source_target_pairs={{0,2},{1,3},{2,0},{3,1},{4,6},{5,7},{6,4},{7,5}} | collective-permute-start | bytes 1572872 | tf_op jit(solution)/shard_map/ppermute | solution.py:274
  74.3 29.7 %collective-permute-start.2 = (bf16[256,1024]{1,0:T(8,128)(2,1)}, bf16[256,1024]{1,0:T(8,128)(2,1)S(1)}, u32[]{:S(2)}, u32[]{:S(2)}) collective-permute-start(bf16[256,1024]{1,0:T(8,128)(2,1)} %shard_map.100.rest_0_.rest_1_), channel_id=1, source_target_pairs={{0,1},{1,0},{2,3},{3,2},{4,5},{5,4},{6,7},{7,6}} | collective-permute-start | bytes 1572872 | tf_op jit(solution)/shard_map/ppermute | solution.py:274
  92.2 42.1 %collective-permute-start.7 = (bf16[256,1024]{1,0:T(8,128)(2,1)}, bf16[256,1024]{1,0:T(8,128)(2,1)S(1)}, u32[]{:S(2)}, u32[]{:S(2)}) collective-permute-start(bf16[256,1024]{1,0:T(8,128)(2,1)} %shard_map.101.rest_8_.rest_9_), channel_id=1, source_target_pairs={{0,2},{1,3},{2,0},{3,1},{4,6},{5,7},{6,4},{7,5}} | collective-permute-start | bytes 1572872 | tf_op jit(solution)/shard_map/ppermute | solution.py:274
  92.6 11.5 %collective-permute-start.4 = (bf16[256,1024]{1,0:T(8,128)(2,1)S(1)}, bf16[256,1024]{1,0:T(8,128)(2,1)S(1)}, u32[]{:S(2)}, u32[]{:S(2)}) collective-permute-start(bf16[256,1024]{1,0:T(8,128)(2,1)S(1)} %collective-permute-done.3.rest_4_.rest_5_), channel_id=1, source_target_pairs={{0,1},{1,0},{2,3},{3,2},{4,5},{5,4},{6,7},{7,6}} | collective-permute-start | bytes 1572872 | tf_op jit(solution)/shard_map/ppermute | solution.py:274
  130.7 58.6 %collective-permute-start.5 = (f32[128,5120]{1,0:T(8,128)}, f32[128,5120]{1,0:T(8,128)}, u32[]{:S(2)}, u32[]{:S(2)}) collective-permute-start(f32[128,5120]{1,0:T(8,128)} %get-tuple-element.56), channel_id=1, source_target_pairs={{0,4},{4,0},{1,5},{5,1},{2,6},{6,2},{3,7},{7,3}} | collective-permute-start | bytes 7864328 | tf_op jit(solution)/shard_map/ppermute | solution.py:271
  192.3 31.7 %collective-permute-start.9 = (bf16[128,5120]{1,0:T(8,128)(2,1)S(1)}, bf16[128,5120]{1,0:T(8,128)(2,1)S(1)}, u32[]{:S(2)}, u32[]{:S(2)}) collective-permute-start(bf16[128,5120]{1,0:T(8,128)(2,1)S(1)} %fusion.22.a_ref), channel_id=1, source_target_pairs={{0,4},{4,0},{1,5},{5,1},{2,6},{6,2},{3,7},{7,3}} | collective-permute-start | bytes 3932168 | tf_op jit(solution)/shard_map/ppermute | solution.py:271
  194.0 86.2 %collective-permute-start.10 = (f32[128,5120]{1,0:T(8,128)}, f32[128,5120]{1,0:T(8,128)}, u32[]{:S(2)}, u32[]{:S(2)}) collective-permute-start(f32[128,5120]{1,0:T(8,128)} %get-tuple-element.63), channel_id=1, source_target_pairs={{0,4},{4,0},{1,5},{5,1},{2,6},{6,2},{3,7},{7,3}} | collective-permute-start | bytes 7864328 | tf_op jit(solution)/shard_map/ppermute | solution.py:271
  283.9 34.0 %collective-permute-start.12 = (bf16[128,5120]{1,0:T(8,128)(2,1)S(1)}, bf16[128,5120]{1,0:T(8,128)(2,1)}, u32[]{:S(2)}, u32[]{:S(2)}) collective-permute-start(bf16[128,5120]{1,0:T(8,128)(2,1)S(1)} %fusion.26.a_ref), channel_id=1, source_target_pairs={{0,4},{4,0},{1,5},{5,1},{2,6},{6,2},{3,7},{7,3}} | collective-permute-start | bytes 3932168 | tf_op jit(solution)/shard_map/ppermute | solution.py:271
  317.5 58.8 %collective-permute-start.11 = (f32[128,5120]{1,0:T(8,128)}, f32[128,5120]{1,0:T(8,128)}, u32[]{:S(2)}, u32[]{:S(2)}) collective-permute-start(f32[128,5120]{1,0:T(8,128)} %get-tuple-element.67), channel_id=1, source_target_pairs={{0,4},{4,0},{1,5},{5,1},{2,6},{6,2},{3,7},{7,3}} | collective-permute-start | bytes 7864328 | tf_op jit(solution)/shard_map/ppermute | solution.py:271
  379.2 29.9 %collective-permute-start.13 = (bf16[128,5120]{1,0:T(8,128)(2,1)S(1)}, bf16[128,5120]{1,0:T(8,128)(2,1)S(1)}, u32[]{:S(2)}, u32[]{:S(2)}) collective-permute-start(bf16[128,5120]{1,0:T(8,128)(2,1)S(1)} %fusion.30.a_ref), channel_id=1, source_target_pairs={{0,4},{4,0},{1,5},{5,1},{2,6},{6,2},{3,7},{7,3}} | collective-permute-start | bytes 3932168 | tf_op jit(solution)/shard_map/ppermute | solution.py:271
  417.7 37.4 %collective-permute-start.15 = (bf16[256,1024]{1,0:T(8,128)(2,1)}, bf16[256,1024]{1,0:T(8,128)(2,1)S(1)}, u32[]{:S(2)}, u32[]{:S(2)}) collective-permute-start(bf16[256,1024]{1,0:T(8,128)(2,1)} %shard_map.109.rest_0_.rest_1_), channel_id=1, source_target_pairs={{0,2},{1,3},{2,0},{3,1},{4,6},{5,7},{6,4},{7,5}} | collective-permute-start | bytes 1572872 | tf_op jit(solution)/shard_map/ppermute | solution.py:274
  454.4 56.7 %collective-permute-start.17 = (f32[128,5120]{1,0:T(8,128)}, f32[128,5120]{1,0:T(8,128)}, u32[]{:S(2)}, u32[]{:S(2)}) collective-permute-start(f32[128,5120]{1,0:T(8,128)} %get-tuple-element.75), channel_id=1, source_target_pairs={{0,4},{4,0},{1,5},{5,1},{2,6},{6,2},{3,7},{7,3}} | collective-permute-start | bytes 7864328 | tf_op jit(solution)/shard_map/ppermute | solution.py:271
  455.1 10.6 %collective-permute-start.16 = (bf16[256,1024]{1,0:T(8,128)(2,1)S(1)}, bf16[256,1024]{1,0:T(8,128)(2,1)S(1)}, u32[]{:S(2)}, u32[]{:S(2)}) collective-permute-start(bf16[256,1024]{1,0:T(8,128)(2,1)S(1)} %collective-permute-done.15.rest_4_.rest_5_), channel_id=1, source_target_pairs={{0,1},{1,0},{2,3},{3,2},{4,5},{5,4},{6,7},{7,6}} | collective-permute-start | bytes 1572872 | tf_op jit(solution)/shard_map/ppermute | solution.py:274
  514.8 27.9 %collective-permute-start.19 = (bf16[128,5120]{1,0:T(8,128)(2,1)S(1)}, bf16[128,5120]{1,0:T(8,128)(2,1)S(1)}, u32[]{:S(2)}, u32[]{:S(2)}) collective-permute-start(bf16[128,5120]{1,0:T(8,128)(2,1)S(1)} %fusion.34.a_ref), channel_id=1, source_target_pairs={{0,4},{4,0},{1,5},{5,1},{2,6},{6,2},{3,7},{7,3}} | collective-permute-start | bytes 3932168 | tf_op jit(solution)/shard_map/ppermute | solution.py:271
  551.8 57.9 %collective-permute-start.18 = (f32[128,5120]{1,0:T(8,128)}, f32[128,5120]{1,0:T(8,128)}, u32[]{:S(2)}, u32[]{:S(2)}) collective-permute-start(f32[128,5120]{1,0:T(8,128)} %get-tuple-element.77), channel_id=1, source_target_pairs={{0,4},{4,0},{1,5},{5,1},{2,6},{6,2},{3,7},{7,3}} | collective-permute-start | bytes 7864328 | tf_op jit(solution)/shard_map/ppermute | solution.py:271
  552.7 19.6 %collective-permute-start.20 = (bf16[256,1024]{1,0:T(8,128)(2,1)}, bf16[256,1024]{1,0:T(8,128)(2,1)S(1)}, u32[]{:S(2)}, u32[]{:S(2)}) collective-permute-start(bf16[256,1024]{1,0:T(8,128)(2,1)} %shard_map.113.rest_8_.rest_9_), channel_id=1, source_target_pairs={{0,1},{1,0},{2,3},{3,2},{4,5},{5,4},{6,7},{7,6}} | collective-permute-start | bytes 1572872 | tf_op jit(solution)/shard_map/ppermute | solution.py:274
  561.4 10.9 %collective-permute-start.22 = (bf16[256,1024]{1,0:T(8,128)(2,1)S(1)}, bf16[256,1024]{1,0:T(8,128)(2,1)S(1)}, u32[]{:S(2)}, u32[]{:S(2)}) collective-permute-start(bf16[256,1024]{1,0:T(8,128)(2,1)S(1)} %collective-permute-done.21.rest_12_.rest_13_), channel_id=1, source_target_pairs={{0,1},{1,0},{2,3},{3,2},{4,5},{5,4},{6,7},{7,6}} | collective-permute-start | bytes 1572872 | tf_op jit(solution)/shard_map/ppermute | solution.py:274
  613.6 31.7 %collective-permute-start.23 = (bf16[128,5120]{1,0:T(8,128)(2,1)S(1)}, bf16[128,5120]{1,0:T(8,128)(2,1)}, u32[]{:S(2)}, u32[]{:S(2)}) collective-permute-start(bf16[128,5120]{1,0:T(8,128)(2,1)S(1)} %fusion.38.a_ref), channel_id=1, source_target_pairs={{0,4},{4,0},{1,5},{5,1},{2,6},{6,2},{3,7},{7,3}} | collective-permute-start | bytes 3932168 | tf_op jit(solution)/shard_map/ppermute | solution.py:271
  614.7 85.6 %collective-permute-start.24 = (f32[128,5120]{1,0:T(8,128)}, f32[128,5120]{1,0:T(8,128)S(1)}, u32[]{:S(2)}, u32[]{:S(2)}) collective-permute-start(f32[128,5120]{1,0:T(8,128)} %get-tuple-element.83), channel_id=1, source_target_pairs={{0,4},{4,0},{1,5},{5,1},{2,6},{6,2},{3,7},{7,3}} | collective-permute-start | bytes 7864328 | tf_op jit(solution)/shard_map/ppermute | solution.py:271
  702.5 33.9 %collective-permute-start.26 = (bf16[128,5120]{1,0:T(8,128)(2,1)S(1)}, bf16[128,5120]{1,0:T(8,128)(2,1)}, u32[]{:S(2)}, u32[]{:S(2)}) collective-permute-start(bf16[128,5120]{1,0:T(8,128)(2,1)S(1)} %fusion.42.a_ref), channel_id=1, source_target_pairs={{0,4},{4,0},{1,5},{5,1},{2,6},{6,2},{3,7},{7,3}} | collective-permute-start | bytes 3932168 | tf_op jit(solution)/shard_map/ppermute | solution.py:271
  735.4 55.9 %collective-permute-start.25 = (f32[128,5120]{1,0:T(8,128)}, f32[128,5120]{1,0:T(8,128)S(1)}, u32[]{:S(2)}, u32[]{:S(2)}) collective-permute-start(f32[128,5120]{1,0:T(8,128)} %get-tuple-element.87), channel_id=1, source_target_pairs={{0,4},{4,0},{1,5},{5,1},{2,6},{6,2},{3,7},{7,3}} | collective-permute-start | bytes 7864328 | tf_op jit(solution)/shard_map/ppermute | solution.py:271
  823.6 55.1 %collective-permute-start.27 = (f32[128,5120]{1,0:T(8,128)}, f32[128,5120]{1,0:T(8,128)S(1)}, u32[]{:S(2)}, u32[]{:S(2)}) collective-permute-start(f32[128,5120]{1,0:T(8,128)} %get-tuple-element.92), channel_id=1, source_target_pairs={{0,4},{4,0},{1,5},{5,1},{2,6},{6,2},{3,7},{7,3}} | collective-permute-start | bytes 7864328 | tf_op jit(solution)/shard_map/ppermute | solution.py:271
  (56 other events, 1308.4 us)
